TPU v7x, 256 devices: a 8x8x2 block of a 8x8x16 slice. The times are simulated.
256 devices in a mesh: groups: 2 (over z), seq: 128 (over x, y, core).
Axes of the slice: x: 8, y: 8, z: 2, core: 2. Of those that a mesh axis runs over, the one named last changes fastest.
The devices are a block of a 8x8x16 slice.
Arguments:
- queries: bfloat16 [64, 128, 576], P('groups', 'seq'), parts along dimension 0, may hold values from -8 to 8
- prefix_pool: bfloat16 [8192, 64, 576], P(('groups', 'seq')), parts along dimension 0, may hold values from -6 to 6
- block_table: int32 [8, 1024], P('groups'), parts along dimension 0, may hold values from 0 to 4095, as said below
- prefix_of: int32 [64], P('groups'), parts along dimension 0, may hold values from 0 to 3
- suffix_cache: bfloat16 [64, 16384, 576], P('groups', 'seq'), parts along dimension 0, may hold values from -24 to 24
- suffix_len: int32 [64], P('groups'), parts along dimension 0, may hold values from 2 to 16384
Outputs:
- context: bfloat16 [64, 128, 512], P('groups', 'seq'), parts along dimension 0
There are 2 independent parts, one for each index of `groups`. A program takes and returns all parts, laid end to end along the dimension named above; each array names one. Nothing has to cross between parts.
Inputs may be any that keep to these rules, and one draw needn't show every extreme that they name: `block_table`: each of the 4096 pool blocks is named exactly once in the table, and of each aligned run of 32 pool blocks exactly 8 belong to each prefix.
All inputs are finite; a program needn't handle non-finite values.
Results may differ from a plain program's by a relative error of at most 0.0033.
Values may be sent and summed in bfloat16 or wider, within the bound.
No kernel may reach another device: no remote copies, remote signals or barrier semaphores. Data moves between devices by JAX's collectives and lax.ppermute only.
A program may use at most 128 MiB of HBM per device.

v0:
```python
import functools
import math

import jax
import jax.numpy as jnp
from jax import lax
from jax.experimental import pallas as pl
from jax.experimental.pallas import tpu as pltpu
from jax.sharding import PartitionSpec as P


LAT = 512
PARTS = 2
WIDE = 2
CORES = 2
LOG2_SCALE = math.log2(math.e) * 192.0 ** (-0.5)
VMEM = pl.BlockSpec(memory_space=pltpu.VMEM)
SMEM = pl.BlockSpec(memory_space=pltpu.SMEM)
ANY = pl.BlockSpec(memory_space=pl.ANY)


class Torus:
    def __init__(self, devices):
        self.devices = devices
        self.side = math.isqrt(devices // CORES)

    def at(self, x, y, core):
        return ((x % self.side) * self.side + y % self.side) * CORES + core

    def groups(self, first):
        n = self.side
        along_x = [[[self.at(x, y, c) for x in range(n)] for y in range(n)] for c in range(CORES)]
        along_y = [[[self.at(x, y, c) for y in range(n)] for x in range(n)] for c in range(CORES)]
        return along_x[0] + along_y[1] if first else along_y[0] + along_x[1]

    def shift(self, value, by):
        n, pairs = self.side, []
        for x in range(n):
            for y in range(n):
                pairs.append((self.at(x, y, 0), self.at(x, y + by, 0)))
                pairs.append((self.at(x, y, 1), self.at(x + by, y, 1)))
        return lax.ppermute(value, "seq", pairs)

    def partner(self, value):
        return lax.ppermute(value, "seq", [(i, i ^ 1) for i in range(self.devices)])


def stage_kernel(core_ref, label_ref, own_pool, other_pool, out, keys, counts, sems):
    prefixes = keys.shape[0]
    held, rows, _ = own_pool.shape
    core = core_ref[0]
    for p in range(prefixes):
        counts[p] = 0

    def place(source, first):
        def step(b, carry):
            p = label_ref[first + b]
            at = counts[p]
            counts[p] = at + 1
            start = pl.multiple_of(at * rows, rows)
            pltpu.make_async_copy(source.at[b], keys.at[p, pl.ds(start, rows)], sems.at[p]).start()
            return carry

        lax.fori_loop(0, held, step, 0)

    place(own_pool, core * held)
    place(other_pool, (1 - core) * held)
    copies = []
    for p in range(prefixes):
        pltpu.make_async_copy(keys.at[p], keys.at[p], sems.at[p]).wait()
        copies.append(pltpu.make_async_copy(keys.at[p], out.at[p], sems.at[prefixes + p]))
        copies[p].start()
    for copy in copies:
        copy.wait()


def attend_kernel(core_ref, prefix_ref, live_ref, sorted_keys, own_suffix, other_suffix, *refs):
    *refs, keys, tails, stat_m, stat_l, heads, members, counts, key_sems, tail_sems = refs
    n = len(refs) // 2
    halved = n // 2
    half = prefix_ref.shape[0] // CORES // 2
    blocks, outs = refs[: len(refs) - n], refs[len(refs) - n :]
    prefixes = keys.shape[0]
    requests, _, spots = tails.shape
    slots = spots // CORES
    per = outs[0].shape[1]
    total = n * per
    core = core_ref[0]

    for p in range(prefixes):
        counts[p] = 0

    def sort(r, carry):
        p = prefix_ref[core * requests + r]
        at = counts[p]
        members[p * requests + at] = r
        counts[p] = at + 1
        return carry

    lax.fori_loop(0, requests, sort, 0)

    def key_copy(p):
        return pltpu.make_async_copy(sorted_keys.at[p], keys.at[p], key_sems.at[p])

    def load(p, carry):
        key_copy(p).start()

        def tail(i, carry):
            r = members[p * requests + i]
            mine, theirs = tails.at[r, :, pl.ds(0, slots)], tails.at[r, :, pl.ds(slots, slots)]
            pltpu.make_async_copy(own_suffix.at[core * requests + r], mine, tail_sems.at[r]).start()
            pltpu.make_async_copy(other_suffix.at[core * requests + r], theirs, tail_sems.at[r]).start()
            return carry

        lax.fori_loop(0, counts[p], tail, 0)
        return carry

    lax.fori_loop(0, prefixes, load, 0)
    stat_m[...] = jnp.zeros_like(stat_m)
    stat_l[...] = jnp.ones_like(stat_l)
    nt = (((1,), (1,)), ((), ()))

    def fetch(r, base):
        for k in range(n):
            span = pl.ds(base + k * per, per)
            if k != halved:
                heads[span] = blocks[k][r]
                continue

            @pl.when(r < half)
            def _():
                heads[span] = blocks[k][r]

            @pl.when(r >= half)
            def _():
                heads[span] = blocks[n][r - half]

    def split(w):
        high = w.astype(jnp.bfloat16)
        low = (w - high.astype(jnp.float32)).astype(jnp.bfloat16)
        return jnp.concatenate([high, low], axis=0)

    def group(p, i):
        last = counts[p] - 1
        rs = [members[p * requests + jnp.minimum(WIDE * i + j, last)] for j in range(WIDE)]
        for j in range(WIDE):
            fetch(rs[j], j * total)

            @pl.when(WIDE * i + j <= last)
            def _():
                pltpu.make_async_copy(tails.at[rs[j]], tails.at[rs[j]], tail_sems.at[rs[j]]).wait()

        q = heads[...]
        cuts = keys.shape[1] // PARTS
        fronts, tops = [], []
        for c in range(PARTS):
            part = keys[p, c * cuts : (c + 1) * cuts]
            f = lax.dot_general(q, part, nt, preferred_element_type=jnp.float32)
            fronts.append(f)
            tops.append(jnp.max(f, axis=1, keepdims=True))
        slot = lax.broadcasted_iota(jnp.int32, (total, spots), 1)
        o, sums = None, None
        best = functools.reduce(jnp.maximum, tops)
        ends, edge = [], []
        for j in range(WIDE):
            s = jnp.dot(q[j * total : (j + 1) * total], tails[rs[j]], preferred_element_type=jnp.float32)
            mine, theirs = live_ref[rs[j]], live_ref[requests + rs[j]]
            limit = jnp.where(slot < slots, mine, theirs + slots)
            s = jnp.where(slot < limit, s, -jnp.inf)
            ends.append(s)
            edge.append(jnp.max(s, axis=1, keepdims=True))
        top = jnp.maximum(best, jnp.concatenate(edge, axis=0)).astype(jnp.bfloat16).astype(jnp.float32)
        for c in range(PARTS):
            w = jnp.exp2((fronts[c] - tops[c]) * LOG2_SCALE)
            fix = jnp.exp2((tops[c] - top) * LOG2_SCALE)
            t = jnp.dot(split(w), keys[p, c * cuts : (c + 1) * cuts, :LAT], preferred_element_type=jnp.float32)
            t = (t[: WIDE * total] + t[WIDE * total :]) * fix
            l = jnp.sum(w, axis=1, keepdims=True) * fix
            o, sums = (t, l) if o is None else (o + t, sums + l)
        for j in range(WIDE):
            r = rs[j]
            here = slice(j * total, (j + 1) * total)
            w = jnp.exp2((ends[j] - top[here]) * LOG2_SCALE)
            l = sums[here] + jnp.sum(w, axis=1, keepdims=True)
            t = lax.dot_general(split(w), tails[r, :LAT], nt, preferred_element_type=jnp.float32)
            res = o[here] + t[:total] + t[total:]
            for k in range(n):
                outs[k][r] = res[k * per : (k + 1) * per].astype(outs[k].dtype)
            lane = lax.broadcasted_iota(jnp.int32, stat_m.shape, 1)
            stat_m[...] = jnp.where(lane == r, top[here], stat_m[...])
            stat_l[...] = jnp.where(lane == r, l, stat_l[...])

    def prefix(p, carry):
        key_copy(p).wait()
        lax.fori_loop(0, (counts[p] + WIDE - 1) // WIDE, lambda i, c: (group(p, i), c)[1], 0)
        return carry

    lax.fori_loop(0, prefixes, prefix, 0)

    for k in range(n):
        here = slice(k * per, (k + 1) * per)
        l = stat_l[here]
        high = l.astype(jnp.bfloat16).astype(jnp.float32)
        parts = [stat_m[here], high, l - high, jnp.zeros_like(l)]
        outs[k][requests] = jnp.concatenate(parts, axis=1).astype(outs[k].dtype)


def merge_kernel(*refs):
    parts, out = refs[:-1], refs[-1]
    requests = parts[0].shape[0] - 1
    per = parts[0].shape[1]
    stats = [p[requests].astype(jnp.float32) for p in parts]
    lanes = 128
    tops = [s[:, :lanes] for s in stats]
    sums = [s[:, lanes : 2 * lanes] + s[:, 2 * lanes : 3 * lanes] for s in stats]
    top = functools.reduce(jnp.maximum, tops)
    scales = [jnp.exp2((t - top) * LOG2_SCALE) for t in tops]
    l = functools.reduce(jnp.add, [s * f for s, f in zip(sums, scales)])
    lane = lax.broadcasted_iota(jnp.int32, (per, lanes), 1)
    for r in range(requests):
        acc = None
        for part, f in zip(parts, scales):
            term = part[r].astype(jnp.float32) * f[:, r : r + 1]
            acc = term if acc is None else acc + term
        out[:, r, :LAT] = acc
        out[:, r, LAT:] = jnp.where(lane == 0, top[:, r : r + 1], l[:, r : r + 1])


def finish_kernel(parts, out):
    peers = parts.shape[0]
    for h in range(parts.shape[1]):
        tops = [parts[j, h, :, LAT : LAT + 1] for j in range(peers)]
        top = functools.reduce(jnp.maximum, tops)
        acc, l = None, None
        for j in range(peers):
            f = jnp.exp2((tops[j] - top) * LOG2_SCALE)
            a = parts[j, h, :, :LAT] * f
            b = parts[j, h, :, LAT + 1 : LAT + 2] * f
            acc, l = (a, b) if acc is None else (acc + a, l + b)
        out[h] = (acc / l).astype(out.dtype)


def stage(core, labels, own_pool, other_pool, prefixes):
    held, rows, channels = own_pool.shape
    keys = (prefixes, CORES * held // prefixes * rows, channels)
    own_pool = pltpu.with_memory_space_constraint(own_pool, pltpu.HBM)
    return pl.pallas_call(
        stage_kernel,
        out_shape=pltpu.HBM(keys, jnp.bfloat16),
        in_specs=[SMEM] * 2 + [ANY] * 2,
        out_specs=ANY,
        scratch_shapes=[
            pltpu.VMEM(keys, jnp.bfloat16),
            pltpu.SMEM((prefixes,), jnp.int32),
            pltpu.SemaphoreType.DMA((2 * prefixes,)),
        ],
        compiler_params=pltpu.CompilerParams(vmem_limit_bytes=8 * 2**20),
        cost_estimate=pl.CostEstimate(flops=4 * 10**9, bytes_accessed=0, transcendentals=0),
        name="stage",
    )(core, labels, own_pool, other_pool)


def attend(core, prefix_of, live, keys, own_suffix, other_suffix, blocks, dtypes):
    n = len(dtypes)
    half, per, channels = blocks[0].shape
    prefixes = keys.shape[0]
    tails = (half, channels, CORES * other_suffix.shape[2])
    flops = 6 * half * n * per * channels * (keys.shape[1] + tails[2])
    keys, own_suffix, other_suffix = (
        pltpu.with_memory_space_constraint(a, pltpu.HBM) for a in (keys, own_suffix, other_suffix)
    )
    return pl.pallas_call(
        attend_kernel,
        out_shape=[jax.ShapeDtypeStruct((half + 1, per, LAT), t) for t in dtypes],
        in_specs=[SMEM] * 3 + [ANY] * 3 + [VMEM] * len(blocks),
        out_specs=[VMEM] * n,
        scratch_shapes=[
            pltpu.VMEM(keys.shape, jnp.bfloat16),
            pltpu.VMEM(tails, jnp.bfloat16),
            pltpu.VMEM((n * per, 128), jnp.float32),
            pltpu.VMEM((n * per, 128), jnp.float32),
            pltpu.VMEM((WIDE * n * per, channels), jnp.bfloat16),
            pltpu.SMEM((prefixes * half,), jnp.int32),
            pltpu.SMEM((prefixes,), jnp.int32),
            pltpu.SemaphoreType.DMA((prefixes,)),
            pltpu.SemaphoreType.DMA((half,)),
        ],
        compiler_params=pltpu.CompilerParams(vmem_limit_bytes=36 * 2**20),
        cost_estimate=pl.CostEstimate(flops=flops, bytes_accessed=0, transcendentals=0),
        name="attend",
    )(core, prefix_of, live, keys, own_suffix, other_suffix, *blocks)


def body(torus, queries, prefix_pool, block_table, prefix_of, suffix_cache, suffix_len):
    side = torus.side
    held, _, channels = prefix_pool.shape
    prefixes = block_table.shape[0]
    reqs, slots, _ = suffix_cache.shape
    half = reqs // CORES
    position = lax.axis_index("seq")
    core = position % CORES

    q = queries.reshape(CORES, half, channels)
    mine, theirs = q[core], q[1 - core]
    theirs = torus.partner(theirs)
    suffix = jnp.swapaxes(suffix_cache, 1, 2)
    pool, theirs = lax.optimization_barrier((prefix_pool, theirs))
    pair_q = jnp.stack([mine, theirs])
    other_pool = torus.partner(pool)
    other_suffix = torus.partner(suffix)

    first_block = (position - core) * held
    ids = first_block + lax.iota(jnp.int32, CORES * held)
    named = jnp.any(block_table[:, :, None] == ids[None, None, :], axis=1)
    labels = jnp.sum(named.astype(jnp.int32) * lax.iota(jnp.int32, prefixes)[:, None], axis=0)
    lengths = lax.dynamic_slice_in_dim(suffix_len, core * half, half, 0)
    live = jnp.concatenate([lengths - position * slots, lengths - (position ^ 1) * slots])

    spread = jnp.broadcast_to(pair_q[None], (side,) + pair_q.shape)
    line = lax.all_to_all(spread, "seq", 0, 0, axis_index_groups=torus.groups(True))
    per = side * CORES
    block = jnp.swapaxes(line.reshape(per, half, channels), 0, 1)

    order = (4, 3, side - 3, 2, side - 2, 1, side - 1)
    got = {0: block}
    mid = half // 2
    for k in (2, side - 2, 1, side - 1):
        got[k] = torus.shift(block, k)
    got[4] = torus.shift(got[2][:mid], 2)
    got[side] = torus.shift(got[side - 2][mid:], side - 2)
    got[3] = torus.shift(got[2], 1)
    got[side - 3] = torus.shift(got[side - 2], side - 1)

    core = core.reshape(1)
    keys = stage(core, labels, prefix_pool, other_pool, prefixes)
    types = [jnp.float32] + [jnp.bfloat16] * (side - 1)
    outs = attend(core, prefix_of, live, keys, suffix, other_suffix, [got[k] for k in range(side + 1)], types)
    parts = [outs[0]] + [torus.shift(outs[k], side - k) for k in order]
    merged = pl.pallas_call(
        merge_kernel,
        out_shape=jax.ShapeDtypeStruct((per, half, LAT + 128), jnp.float32),
        in_specs=[VMEM] * side,
        out_specs=VMEM,
        compiler_params=pltpu.CompilerParams(vmem_limit_bytes=16 * 2**20),
        name="merge",
    )(*parts)
    shares = lax.all_to_all(
        merged.reshape(side, CORES, half, LAT + 128), "seq", 0, 0, axis_index_groups=torus.groups(True)
    )
    context = pl.pallas_call(
        finish_kernel,
        out_shape=jax.ShapeDtypeStruct((CORES, half, LAT), jnp.bfloat16),
        in_specs=[VMEM],
        out_specs=VMEM,
        compiler_params=pltpu.CompilerParams(vmem_limit_bytes=8 * 2**20),
        name="finish",
    )(shares)
    back = torus.partner(context[1])
    both = jnp.where(core[0] == 0, jnp.stack([context[0], back]), jnp.stack([back, context[0]]))
    return both.reshape(reqs, 1, LAT)


def solution(mesh):
    torus = Torus(mesh.shape["seq"])

    def step(*args):
        return body(torus, *args)

    return jax.shard_map(
        step,
        mesh=mesh,
        in_specs=(
            P("groups", "seq", None),
            P(("groups", "seq"), None, None),
            P("groups", None),
            P("groups"),
            P("groups", "seq", None),
            P("groups"),
        ),
        out_specs=P("groups", "seq", None),
        check_vma=False,
    )
```

profile of v0, /device:TPU:513, one launch (start us, length us, event | category | flops | bytes accessed | tf_op | source)
XLA Modules:
  0.0 138.6 jit_solution(15536208981533362805)
XLA Ops:
  0.0 20.4 %collective-permute-start.2 = (bf16[32,576,128]{2,1,0:T(8,128)(2,1)}, bf16[32,576,128]{2,1,0:T(8,128)(2,1)}, u32[]{:S(2)}, u32[]{:S(2)}) collective-permute-start(bf16[32,576,128]{2,1,0:T(8,128)(2,1)} %bitcast.23), channel_id=1, source_target_pairs={{0,1},{1,0},{2,3},{3,2},{4,5},{5,4},{6,7},{7,6},{8,9},{9,8},{10,11... | collective-permute-start | bytes 14155784 | tf_op jit(solution)/shard_map/ppermute | solution.py:45
  20.4 0.7 constant_dynamic-slice_fusion
  21.2 7.1 %collective-permute-done = bf16[16,576]{1,0:T(8,128)(2,1)S(1)} collective-permute-done((bf16[16,576]{1,0:T(8,128)(2,1)S(1)}, bf16[16,576]{1,0:T(8,128)(2,1)S(1)}, u32[]{:S(2)}, u32[]{:S(2)}) %collective-permute-start) | collective-permute-done | bytes 18464 | tf_op jit(solution)/shard_map/ppermute | solution.py:45
  28.3 0.4 collective-permute-start.1
  28.9 12.5 %all_to_all.10 = bf16[8,2,16,576]{3,1,2,0:T(2,128)(2,1)S(1)} all-to-all(bf16[8,2,16,576]{3,1,2,0:T(2,128)(2,1)S(1)} %broadcast_in_dim.2), channel_id=1, replica_groups={{0,16,32,48,64,80,96,112},{2,18,34,50,66,82,98,114},{4,20,36,52,68,84,1..., dimensions={0} | all-to-all | bytes 589824 | tf_op jit(solution)/shard_map/all_to_all | solution.py:320
  42.0 0.7 broadcast_subtract_fusion.1
  42.7 2.3 %collective-permute-start.4 = (bf16[16,16,576]{2,1,0:T(8,128)(2,1)S(1)}, bf16[16,16,576]{2,1,0:T(8,128)(2,1)S(1)}, u32[]{:S(2)}, u32[]{:S(2)}) collective-permute-start(bf16[16,16,576]{2,1,0:T(8,128)(2,1)S(1)} %bitcast.16), channel_id=1, source_target_pairs={{0,4},{1,33},{2,6},{3,35},{4,8},{5,37},{6,10},{7,39},{8,12},{9,41}... | collective-permute-start | bytes 884744 | tf_op jit(solution)/shard_map/ppermute | solution.py:42
  45.1 4.1 %collective-permute-done.7.refs_6_ = bf16[16,16,576]{2,1,0:T(8,128)(2,1)S(1)} collective-permute-done((bf16[16,16,576]{2,1,0:T(8,128)(2,1)S(1)}, bf16[16,16,576]{2,1,0:T(8,128)(2,1)S(1)}, u32[]{:S(2)}, u32[]{:S(2)}) %collective-permute-start.7) | collective-permute-done | bytes 294944 | tf_op jit(solution)/shard_map/ppermute | solution.py:42
  49.2 1.0 compare_reduce_fusion
  50.3 0.8 collective-permute-done.4.refs_2_
  51.1 0.4 collective-permute-start.10
  51.6 3.0 %collective-permute-done.3.refs_1_ = bf16[16,16,576]{2,1,0:T(8,128)(2,1)S(1)} collective-permute-done((bf16[16,16,576]{2,1,0:T(8,128)(2,1)S(1)}, bf16[16,16,576]{2,1,0:T(8,128)(2,1)S(1)}, u32[]{:S(2)}, u32[]{:S(2)}) %collective-permute-start.3) | collective-permute-done | bytes 294944 | tf_op jit(solution)/shard_map/ppermute | solution.py:42
  54.8 1.1 collective-permute-done.9.refs_7_
  56.0 2.7 %collective-permute-start.8 = (bf16[16,16,576]{2,1,0:T(8,128)(2,1)S(1)}, bf16[16,16,576]{2,1,0:T(8,128)(2,1)S(1)}, u32[]{:S(2)}, u32[]{:S(2)}) collective-permute-start(bf16[16,16,576]{2,1,0:T(8,128)(2,1)S(1)} %collective-permute-done.7.refs_6_), channel_id=1, source_target_pairs={{0,14},{1,113},{2,0},{3,115},{4,2},{5,117},{6,4},{7,119},{8,6},{9,... | collective-permute-start | bytes 884744 | tf_op jit(solution)/shard_map/ppermute | solution.py:42
  58.7 7.1 %stage.1.sorted_keys = bf16[4,1024,576]{2,1,0:T(8,128)(2,1)} custom-call(s32[1]{0:T(128)} %bitcast.core_ref, s32[64]{0:T(128)S(1)} %select_reduce_fusion.label_ref, bf16[32,64,576]{2,1,0:T(8,128)(2,1)} %own_pool.1, bf16[32,64,576]{2,1,0:T(8,128)(2,1)S(1)} %collective-permute-done.1.other_pool), custom_call_target="tpu_custom_call" | custom-call | flops 4000000000 | tf_op jit(solution)/shard_map/stage/pallas_call | solution.py:247
  65.9 15.9 %attend.1 = (f32[17,16,512]{2,1,0:T(8,128)S(1)}, bf16[17,16,512]{2,1,0:T(8,128)(2,1)S(1)}, bf16[17,16,512]{2,1,0:T(8,128)(2,1)S(1)}, bf16[17,16,512]{2,1,0:T(8,1...) custom-call(s32[1]{0:T(128)} %bitcast.core_ref, ...), custom_call_target="tpu_custom_call" | custom-call | flops 9059696640 | tf_op jit(solution)/shard_map/attend/pallas_call | solution.py:272
  81.8 0.4 collective-permute-start.11
  82.2 2.7 %collective-permute-start.12 = (bf16[17,16,512]{2,1,0:T(8,128)(2,1)S(1)}, bf16[17,16,512]{2,1,0:T(8,128)(2,1)S(1)}, u32[]{:S(2)}, u32[]{:S(2)}) collective-permute-start(bf16[17,16,512]{2,1,0:T(8,128)(2,1)S(1)} %get-tuple-element.19), channel_id=1, source_target_pairs={{0,10},{1,81},{2,12},{3,83},{4,14},{5,85},{6,0},{7,87},{8,2},{9,89... | collective-permute-start | bytes 835592 | tf_op jit(solution)/shard_map/ppermute | solution.py:42
  84.9 0.6 collective-permute-start.13
  85.5 2.9 %collective-permute-start.14 = (bf16[17,16,512]{2,1,0:T(8,128)(2,1)S(1)}, bf16[17,16,512]{2,1,0:T(8,128)(2,1)S(1)}, u32[]{:S(2)}, u32[]{:S(2)}) collective-permute-start(bf16[17,16,512]{2,1,0:T(8,128)(2,1)S(1)} %get-tuple-element.21), channel_id=1, source_target_pairs={{0,12},{1,97},{2,14},{3,99},{4,0},{5,101},{6,2},{7,103},{8,4},{9,1... | collective-permute-start | bytes 835592 | tf_op jit(solution)/shard_map/ppermute | solution.py:42
  88.4 1.0 collective-permute-start.15
  89.4 5.2 %collective-permute-done.11.refs_1_ = bf16[17,16,512]{2,1,0:T(8,128)(2,1)S(1)} collective-permute-done((bf16[17,16,512]{2,1,0:T(8,128)(2,1)S(1)}, bf16[17,16,512]{2,1,0:T(8,128)(2,1)S(1)}, u32[]{:S(2)}, u32[]{:S(2)}) %collective-permute-start.11) | collective-permute-done | bytes 278560 | tf_op jit(solution)/shard_map/ppermute | solution.py:42
  94.7 4.4 %collective-permute-done.12.refs_2_ = bf16[17,16,512]{2,1,0:T(8,128)(2,1)S(1)} collective-permute-done((bf16[17,16,512]{2,1,0:T(8,128)(2,1)S(1)}, bf16[17,16,512]{2,1,0:T(8,128)(2,1)S(1)}, u32[]{:S(2)}, u32[]{:S(2)}) %collective-permute-start.12) | collective-permute-done | bytes 278560 | tf_op jit(solution)/shard_map/ppermute | solution.py:42
  99.0 1.2 collective-permute-start.17
  100.3 3.0 %collective-permute-done.13.refs_3_ = bf16[17,16,512]{2,1,0:T(8,128)(2,1)S(1)} collective-permute-done((bf16[17,16,512]{2,1,0:T(8,128)(2,1)S(1)}, bf16[17,16,512]{2,1,0:T(8,128)(2,1)S(1)}, u32[]{:S(2)}, u32[]{:S(2)}) %collective-permute-start.13) | collective-permute-done | bytes 278560 | tf_op jit(solution)/shard_map/ppermute | solution.py:42
  103.2 4.3 %collective-permute-done.14.refs_4_ = bf16[17,16,512]{2,1,0:T(8,128)(2,1)S(1)} collective-permute-done((bf16[17,16,512]{2,1,0:T(8,128)(2,1)S(1)}, bf16[17,16,512]{2,1,0:T(8,128)(2,1)S(1)}, u32[]{:S(2)}, u32[]{:S(2)}) %collective-permute-start.14) | collective-permute-done | bytes 278560 | tf_op jit(solution)/shard_map/ppermute | solution.py:42
  107.5 1.4 %collective-permute-done.16.refs_6_ = bf16[17,16,512]{2,1,0:T(8,128)(2,1)S(1)} collective-permute-done((bf16[17,16,512]{2,1,0:T(8,128)(2,1)S(1)}, bf16[17,16,512]{2,1,0:T(8,128)(2,1)S(1)}, u32[]{:S(2)}, u32[]{:S(2)}) %collective-permute-start.16) | collective-permute-done | bytes 278560 | tf_op jit(solution)/shard_map/ppermute | solution.py:42
  109.2 0.7 merge.1
  109.9 16.0 %all_to_all.11.parts = f32[8,2,16,640]{3,2,1,0:T(8,128)S(1)} all-to-all(f32[8,2,16,640]{3,2,1,0:T(8,128)S(1)} %bitcast.14), channel_id=1, replica_groups={{0,16,32,48,64,80,96,112},{2,18,34,50,66,82,98,114},{4,20,36,52,68,84,1..., dimensions={0} | all-to-all | bytes 1310720 | tf_op jit(solution)/shard_map/all_to_all | solution.py:347
  126.1 11.1 %collective-permute-start.18 = (bf16[16,512]{1,0:T(8,128)(2,1)S(1)}, bf16[16,512]{1,0:T(8,128)(2,1)S(1)}, u32[]{:S(2)}, u32[]{:S(2)}) collective-permute-start(bf16[16,512]{1,0:T(8,128)(2,1)S(1)} %get-tuple-element.28), channel_id=1, source_target_pairs={{0,1},{1,0},{2,3},{3,2},{4,5},{5,4},{6,7},{7,6},{8,9},{9,8},{10,11... | collective-permute-start | bytes 49160 | tf_op jit(solution)/shard_map/ppermute | solution.py:45
  137.2 0.8 collective-permute-done.18
  138.0 0.6 maximum_select_fusion
  (29 shorter events, 1.7 us)
Async XLA Ops:
  0.0 65.9 %collective-permute-start.2 = (bf16[32,576,128]{2,1,0:T(8,128)(2,1)}, bf16[32,576,128]{2,1,0:T(8,128)(2,1)}, u32[]{:S(2)}, u32[]{:S(2)}) collective-permute-start(bf16[32,576,128]{2,1,0:T(8,128)(2,1)} %bitcast.23), channel_id=1, source_target_pairs={{0,1},{1,0},{2,3},{3,2},{4,5},{5,4},{6,7},{7,6},{8,9},{9,8},{10,11... | collective-permute-start | bytes 14155784 | tf_op jit(solution)/shard_map/ppermute | solution.py:45
  21.2 7.1 %collective-permute-start = (bf16[16,576]{1,0:T(8,128)(2,1)S(1)}, bf16[16,576]{1,0:T(8,128)(2,1)S(1)}, u32[]{:S(2)}, u32[]{:S(2)}) collective-permute-start(bf16[16,576]{1,0:T(8,128)(2,1)S(1)} %get-tuple-element.26), channel_id=1, source_target_pairs={{0,1},{1,0},{2,3},{3,2},{4,5},{5,4},{6,7},{7,6},{8,9},{9,8},{10,11... | collective-permute-start | bytes 55304 | tf_op jit(solution)/shard_map/ppermute | solution.py:45
  28.3 27.7 %collective-permute-start.1 = (bf16[32,64,576]{2,1,0:T(8,128)(2,1)}, bf16[32,64,576]{2,1,0:T(8,128)(2,1)S(1)}, u32[]{:S(2)}, u32[]{:S(2)}) collective-permute-start(bf16[32,64,576]{2,1,0:T(8,128)(2,1)} %own_pool.1), channel_id=1, source_target_pairs={{0,1},{1,0},{2,3},{3,2},{4,5},{5,4},{6,7},{7,6},{8,9},{9,8},{10,11... | collective-permute-start | bytes 7077896 | tf_op jit(solution)/shard_map/ppermute | solution.py:45
  41.8 7.3 %collective-permute-start.7 = (bf16[16,16,576]{2,1,0:T(8,128)(2,1)S(1)}, bf16[16,16,576]{2,1,0:T(8,128)(2,1)S(1)}, u32[]{:S(2)}, u32[]{:S(2)}) collective-permute-start(bf16[16,16,576]{2,1,0:T(8,128)(2,1)S(1)} %bitcast.15), channel_id=1, source_target_pairs={{0,12},{1,97},{2,14},{3,99},{4,0},{5,101},{6,2},{7,103},{8,4},{9,1... | collective-permute-start | bytes 884744 | tf_op jit(solution)/shard_map/ppermute | solution.py:42
  42.7 8.4 %collective-permute-start.4 = (bf16[16,16,576]{2,1,0:T(8,128)(2,1)S(1)}, bf16[16,16,576]{2,1,0:T(8,128)(2,1)S(1)}, u32[]{:S(2)}, u32[]{:S(2)}) collective-permute-start(bf16[16,16,576]{2,1,0:T(8,128)(2,1)S(1)} %bitcast.16), channel_id=1, source_target_pairs={{0,4},{1,33},{2,6},{3,35},{4,8},{5,37},{6,10},{7,39},{8,12},{9,41}... | collective-permute-start | bytes 884744 | tf_op jit(solution)/shard_map/ppermute | solution.py:42
  45.1 9.5 %collective-permute-start.3 = (bf16[16,16,576]{2,1,0:T(8,128)(2,1)S(1)}, bf16[16,16,576]{2,1,0:T(8,128)(2,1)S(1)}, u32[]{:S(2)}, u32[]{:S(2)}) collective-permute-start(bf16[16,16,576]{2,1,0:T(8,128)(2,1)S(1)} %bitcast.17), channel_id=1, source_target_pairs={{0,2},{1,17},{2,4},{3,19},{4,6},{5,21},{6,8},{7,23},{8,10},{9,25},... | collective-permute-start | bytes 884744 | tf_op jit(solution)/shard_map/ppermute | solution.py:42
  49.2 6.8 %collective-permute-start.9 = (bf16[16,16,576]{2,1,0:T(8,128)(2,1)S(1)}, bf16[16,16,576]{2,1,0:T(8,128)(2,1)S(1)}, u32[]{:S(2)}, u32[]{:S(2)}) collective-permute-start(bf16[16,16,576]{2,1,0:T(8,128)(2,1)S(1)} %bitcast.18), channel_id=1, source_target_pairs={{0,14},{1,113},{2,0},{3,115},{4,2},{5,117},{6,4},{7,119},{8,6},{9,... | collective-permute-start | bytes 884744 | tf_op jit(solution)/shard_map/ppermute | solution.py:42
  51.1 14.7 %collective-permute-start.10 = (bf16[8,16,576]{2,1,0:T(8,128)(2,1)S(1)}, bf16[8,16,576]{2,1,0:T(8,128)(2,1)S(1)}, u32[]{:S(2)}, u32[]{:S(2)}) collective-permute-start(bf16[8,16,576]{2,1,0:T(8,128)(2,1)S(1)} %slice.18), channel_id=1, source_target_pairs={{0,12},{1,97},{2,14},{3,99},{4,0},{5,101},{6,2},{7,103},{8,4},{9,1... | collective-permute-start | bytes 442376 | tf_op jit(solution)/shard_map/ppermute | solution.py:42
  54.6 11.2 %collective-permute-start.6 = (bf16[8,16,576]{2,1,0:T(8,128)(2,1)S(1)}, bf16[8,16,576]{2,1,0:T(8,128)(2,1)S(1)}, u32[]{:S(2)}, u32[]{:S(2)}) collective-permute-start(bf16[8,16,576]{2,1,0:T(8,128)(2,1)S(1)} %slice.17), channel_id=1, source_target_pairs={{0,4},{1,33},{2,6},{3,35},{4,8},{5,37},{6,10},{7,39},{8,12},{9,41}... | collective-permute-start | bytes 442376 | tf_op jit(solution)/shard_map/ppermute | solution.py:42
  56.0 9.9 %collective-permute-start.5 = (bf16[16,16,576]{2,1,0:T(8,128)(2,1)S(1)}, bf16[16,16,576]{2,1,0:T(8,128)(2,1)S(1)}, u32[]{:S(2)}, u32[]{:S(2)}) collective-permute-start(bf16[16,16,576]{2,1,0:T(8,128)(2,1)S(1)} %collective-permute-done.4.refs_2_), channel_id=1, source_target_pairs={{0,2},{1,17},{2,4},{3,19},{4,6},{5,21},{6,8},{7,23},{8,10},{9,25},... | collective-permute-start | bytes 884744 | tf_op jit(solution)/shard_map/ppermute | solution.py:42
  56.0 9.9 %collective-permute-start.8 = (bf16[16,16,576]{2,1,0:T(8,128)(2,1)S(1)}, bf16[16,16,576]{2,1,0:T(8,128)(2,1)S(1)}, u32[]{:S(2)}, u32[]{:S(2)}) collective-permute-start(bf16[16,16,576]{2,1,0:T(8,128)(2,1)S(1)} %collective-permute-done.7.refs_6_), channel_id=1, source_target_pairs={{0,14},{1,113},{2,0},{3,115},{4,2},{5,117},{6,4},{7,119},{8,6},{9,... | collective-permute-start | bytes 884744 | tf_op jit(solution)/shard_map/ppermute | solution.py:42
  58.7 7.2 %copy-start = (s32[32]{0:T(128)S(1)}, s32[32]{0:T(128)}, u32[]{:S(2)}) copy-start(s32[32]{0:T(128)} %prefix_ref.1) | copy-start | bytes 388
  81.8 12.9 %collective-permute-start.11 = (bf16[17,16,512]{2,1,0:T(8,128)(2,1)S(1)}, bf16[17,16,512]{2,1,0:T(8,128)(2,1)S(1)}, u32[]{:S(2)}, u32[]{:S(2)}) collective-permute-start(bf16[17,16,512]{2,1,0:T(8,128)(2,1)S(1)} %get-tuple-element.18), channel_id=1, source_target_pairs={{0,8},{1,65},{2,10},{3,67},{4,12},{5,69},{6,14},{7,71},{8,0},{9,73... | collective-permute-start | bytes 835592 | tf_op jit(solution)/shard_map/ppermute | solution.py:42
  82.2 16.9 %collective-permute-start.12 = (bf16[17,16,512]{2,1,0:T(8,128)(2,1)S(1)}, bf16[17,16,512]{2,1,0:T(8,128)(2,1)S(1)}, u32[]{:S(2)}, u32[]{:S(2)}) collective-permute-start(bf16[17,16,512]{2,1,0:T(8,128)(2,1)S(1)} %get-tuple-element.19), channel_id=1, source_target_pairs={{0,10},{1,81},{2,12},{3,83},{4,14},{5,85},{6,0},{7,87},{8,2},{9,89... | collective-permute-start | bytes 835592 | tf_op jit(solution)/shard_map/ppermute | solution.py:42
  84.9 18.3 %collective-permute-start.13 = (bf16[17,16,512]{2,1,0:T(8,128)(2,1)S(1)}, bf16[17,16,512]{2,1,0:T(8,128)(2,1)S(1)}, u32[]{:S(2)}, u32[]{:S(2)}) collective-permute-start(bf16[17,16,512]{2,1,0:T(8,128)(2,1)S(1)} %get-tuple-element.20), channel_id=1, source_target_pairs={{0,6},{1,49},{2,8},{3,51},{4,10},{5,53},{6,12},{7,55},{8,14},{9,57... | collective-permute-start | bytes 835592 | tf_op jit(solution)/shard_map/ppermute | solution.py:42
  85.5 22.1 %collective-permute-start.14 = (bf16[17,16,512]{2,1,0:T(8,128)(2,1)S(1)}, bf16[17,16,512]{2,1,0:T(8,128)(2,1)S(1)}, u32[]{:S(2)}, u32[]{:S(2)}) collective-permute-start(bf16[17,16,512]{2,1,0:T(8,128)(2,1)S(1)} %get-tuple-element.21), channel_id=1, source_target_pairs={{0,12},{1,97},{2,14},{3,99},{4,0},{5,101},{6,2},{7,103},{8,4},{9,1... | collective-permute-start | bytes 835592 | tf_op jit(solution)/shard_map/ppermute | solution.py:42
  88.4 19.1 %collective-permute-start.15 = (bf16[17,16,512]{2,1,0:T(8,128)(2,1)S(1)}, bf16[17,16,512]{2,1,0:T(8,128)(2,1)S(1)}, u32[]{:S(2)}, u32[]{:S(2)}) collective-permute-start(bf16[17,16,512]{2,1,0:T(8,128)(2,1)S(1)} %get-tuple-element.22), channel_id=1, source_target_pairs={{0,4},{1,33},{2,6},{3,35},{4,8},{5,37},{6,10},{7,39},{8,12},{9,41}... | collective-permute-start | bytes 835592 | tf_op jit(solution)/shard_map/ppermute | solution.py:42
  94.7 14.3 %collective-permute-start.16 = (bf16[17,16,512]{2,1,0:T(8,128)(2,1)S(1)}, bf16[17,16,512]{2,1,0:T(8,128)(2,1)S(1)}, u32[]{:S(2)}, u32[]{:S(2)}) collective-permute-start(bf16[17,16,512]{2,1,0:T(8,128)(2,1)S(1)} %get-tuple-element.23), channel_id=1, source_target_pairs={{0,14},{1,113},{2,0},{3,115},{4,2},{5,117},{6,4},{7,119},{8,6},{9,... | collective-permute-start | bytes 835592 | tf_op jit(solution)/shard_map/ppermute | solution.py:42
  99.0 10.2 %collective-permute-start.17 = (bf16[17,16,512]{2,1,0:T(8,128)(2,1)S(1)}, bf16[17,16,512]{2,1,0:T(8,128)(2,1)S(1)}, u32[]{:S(2)}, u32[]{:S(2)}) collective-permute-start(bf16[17,16,512]{2,1,0:T(8,128)(2,1)S(1)} %get-tuple-element.24), channel_id=1, source_target_pairs={{0,2},{1,17},{2,4},{3,19},{4,6},{5,21},{6,8},{7,23},{8,10},{9,25},... | collective-permute-start | bytes 835592 | tf_op jit(solution)/shard_map/ppermute | solution.py:42
  126.1 11.9 %collective-permute-start.18 = (bf16[16,512]{1,0:T(8,128)(2,1)S(1)}, bf16[16,512]{1,0:T(8,128)(2,1)S(1)}, u32[]{:S(2)}, u32[]{:S(2)}) collective-permute-start(bf16[16,512]{1,0:T(8,128)(2,1)S(1)} %get-tuple-element.28), channel_id=1, source_target_pairs={{0,1},{1,0},{2,3},{3,2},{4,5},{5,4},{6,7},{7,6},{8,9},{9,8},{10,11... | collective-permute-start | bytes 49160 | tf_op jit(solution)/shard_map/ppermute | solution.py:45
where the time goes:
time: 139 us
  starting transfers between devices  46.5 us (33%)
  waiting for transfers between devices  35.6 us (26%)
  blocking collectives  28.4 us (20%)
  Pallas kernels  23.9 us (17%)
  other arithmetic  2.47 us (2%)
  local copies, waits for them, and re-layouts  1.47 us (1%)
    ppermute x4, starting transfers between devices, partner(): return lax.ppermute(value, 'seq', [(i, i ^ 1) for i in range(self.devices)])  31.8 us
    ppermute x15, waiting for transfers between devices, shift(): return lax.ppermute(value, 'seq', pairs)  27.7 us
    all_to_all x1, blocking collectives, body(): lax.all_to_all(merged.reshape(side, CORES, half, LAT + 128), 'seq', 0, 0,...  16 us
    pallas_call x1, Pallas kernels, attend(): pl.pallas_call(attend_kernel, out_shape=[jax.ShapeDtypeStruct((half + 1,...  15.9 us
    ppermute x15, starting transfers between devices, shift(): return lax.ppermute(value, 'seq', pairs)  14.7 us
    all_to_all x1, blocking collectives, body(): lax.all_to_all(spread, 'seq', 0, 0, axis_index_groups=torus.groups(True))  12.5 us
    ppermute x4, waiting for transfers between devices, partner(): return lax.ppermute(value, 'seq', [(i, i ^ 1) for i in range(self.devices)])  7.97 us
    pallas_call x1, Pallas kernels, stage(): pl.pallas_call(stage_kernel, out_shape=pltpu.HBM(keys, jnp.bfloat16), in_...  7.15 us
  transfers between devices with their start and end apart: 19, of which 12 were waited for; matrix products, arithmetic and copies ran while one was open for 2% of the time, Pallas kernels for 5%

commit v1 on v0

--- a/solution.py
+++ b/solution.py
@@ -31,14 +31,14 @@
         n = self.side
         along_x = [[[self.at(x, y, c) for x in range(n)] for y in range(n)] for c in range(CORES)]
         along_y = [[[self.at(x, y, c) for y in range(n)] for x in range(n)] for c in range(CORES)]
-        return along_x[0] + along_y[1] if first else along_y[0] + along_x[1]
+        return along_y[0] + along_x[1] if first else along_x[0] + along_y[1]
 
     def shift(self, value, by):
         n, pairs = self.side, []
         for x in range(n):
             for y in range(n):
-                pairs.append((self.at(x, y, 0), self.at(x, y + by, 0)))
-                pairs.append((self.at(x, y, 1), self.at(x + by, y, 1)))
+                pairs.append((self.at(x, y, 0), self.at(x + by, y, 0)))
+                pairs.append((self.at(x, y, 1), self.at(x, y + by, 1)))
         return lax.ppermute(value, "seq", pairs)
 
     def partner(self, value):

time: 139 us -> 137 us (0.986)
  the two profiles are of different devices: /device:TPU:513 before, /device:TPU:516 now
where the time goes in v1:
time: 137 us; the launch traced here: 135 us
  blocking collectives  45.1 us (33%)
  waiting for transfers between devices  33.1 us (24%)
  starting transfers between devices  29.1 us (21%)
  Pallas kernels  23.4 us (17%)
  other arithmetic  2.47 us (2%)
  local copies, waits for them, and re-layouts  1.47 us (1%)
    ppermute x15, starting transfers between devices, shift(): return lax.ppermute(value, 'seq', pairs)  28.3 us
    ppermute x15, waiting for transfers between devices, shift(): return lax.ppermute(value, 'seq', pairs)  25 us
    all_to_all x1, blocking collectives, body(): lax.all_to_all(spread, 'seq', 0, 0, axis_index_groups=torus.groups(True))  24.1 us
    all_to_all x1, blocking collectives, body(): lax.all_to_all(merged.reshape(side, CORES, half, LAT + 128), 'seq', 0, 0,...  21 us
    pallas_call x1, Pallas kernels, attend(): pl.pallas_call(attend_kernel, out_shape=[jax.ShapeDtypeStruct((half + 1,...  15.4 us
    ppermute x4, waiting for transfers between devices, partner(): return lax.ppermute(value, 'seq', [(i, i ^ 1) for i in range(self.devices)])  8.15 us
    pallas_call x1, Pallas kernels, stage(): pl.pallas_call(stage_kernel, out_shape=pltpu.HBM(keys, jnp.bfloat16), in_...  7.15 us
  transfers between devices with their start and end apart: 19, of which 8 were waited for; matrix products, arithmetic and copies ran while one was open for 2% of the time, Pallas kernels for 5%

profile of v1, /device:TPU:516, one launch (start us, length us, event | category | flops | bytes accessed | tf_op | source)
XLA Modules:
  0.0 134.9 jit_solution(1679969206145012605)
XLA Ops:
  0.0 0.7 constant_dynamic-slice_fusion
  0.8 0.5 collective-permute-start
  1.3 7.0 %collective-permute-done = bf16[16,576]{1,0:T(8,128)(2,1)S(1)} collective-permute-done((bf16[16,576]{1,0:T(8,128)(2,1)S(1)}, bf16[16,576]{1,0:T(8,128)(2,1)S(1)}, u32[]{:S(2)}, u32[]{:S(2)}) %collective-permute-start) | collective-permute-done | bytes 18464 | tf_op jit(solution)/shard_map/ppermute | solution.py:45
  8.4 0.2 broadcast_in_dim.2
  8.6 24.1 %all_to_all.10 = bf16[8,2,16,576]{3,1,2,0:T(2,128)(2,1)S(1)} all-to-all(bf16[8,2,16,576]{3,1,2,0:T(2,128)(2,1)S(1)} %broadcast_in_dim.2), channel_id=1, replica_groups={{0,2,4,6,8,10,12,14},{16,18,20,22,24,26,28,30},{32,34,36,38,40,42,44,46..., dimensions={0} | all-to-all | bytes 589824 | tf_op jit(solution)/shard_map/all_to_all | solution.py:320
  32.8 0.2 copy.13
  33.0 0.2 reshape.40
  33.3 8.8 %collective-permute-start.7 = (bf16[16,16,576]{2,1,0:T(8,128)(2,1)S(1)}, bf16[16,16,576]{2,1,0:T(8,128)(2,1)S(1)}, u32[]{:S(2)}, u32[]{:S(2)}) collective-permute-start(bf16[16,16,576]{2,1,0:T(8,128)(2,1)S(1)} %bitcast.15), channel_id=1, source_target_pairs={{0,96},{1,13},{2,98},{3,15},{4,100},{5,1},{6,102},{7,3},{8,104},{9... | collective-permute-start | bytes 884744 | tf_op jit(solution)/shard_map/ppermute | solution.py:42
  42.0 0.7 broadcast_subtract_fusion.1
  42.8 3.8 %collective-permute-done.7.refs_6_ = bf16[16,16,576]{2,1,0:T(8,128)(2,1)S(1)} collective-permute-done((bf16[16,16,576]{2,1,0:T(8,128)(2,1)S(1)}, bf16[16,16,576]{2,1,0:T(8,128)(2,1)S(1)}, u32[]{:S(2)}, u32[]{:S(2)}) %collective-permute-start.7) | collective-permute-done | bytes 294944 | tf_op jit(solution)/shard_map/ppermute | solution.py:42
  46.7 1.0 compare_reduce_fusion
  47.8 3.1 %collective-permute-done.4.refs_2_ = bf16[16,16,576]{2,1,0:T(8,128)(2,1)S(1)} collective-permute-done((bf16[16,16,576]{2,1,0:T(8,128)(2,1)S(1)}, bf16[16,16,576]{2,1,0:T(8,128)(2,1)S(1)}, u32[]{:S(2)}, u32[]{:S(2)}) %collective-permute-start.4) | collective-permute-done | bytes 294944 | tf_op jit(solution)/shard_map/ppermute | solution.py:42
  50.8 1.5 %collective-permute-start.10 = (bf16[8,16,576]{2,1,0:T(8,128)(2,1)S(1)}, bf16[8,16,576]{2,1,0:T(8,128)(2,1)S(1)}, u32[]{:S(2)}, u32[]{:S(2)}) collective-permute-start(bf16[8,16,576]{2,1,0:T(8,128)(2,1)S(1)} %slice.18), channel_id=1, source_target_pairs={{0,96},{1,13},{2,98},{3,15},{4,100},{5,1},{6,102},{7,3},{8,104},{9... | collective-permute-start | bytes 442376 | tf_op jit(solution)/shard_map/ppermute | solution.py:42
  52.3 1.1 collective-permute-done.3.refs_1_
  53.4 1.7 %collective-permute-start.6 = (bf16[8,16,576]{2,1,0:T(8,128)(2,1)S(1)}, bf16[8,16,576]{2,1,0:T(8,128)(2,1)S(1)}, u32[]{:S(2)}, u32[]{:S(2)}) collective-permute-start(bf16[8,16,576]{2,1,0:T(8,128)(2,1)S(1)} %slice.17), channel_id=1, source_target_pairs={{0,32},{1,5},{2,34},{3,7},{4,36},{5,9},{6,38},{7,11},{8,40},{9,13}... | collective-permute-start | bytes 442376 | tf_op jit(solution)/shard_map/ppermute | solution.py:42
  55.1 2.0 %collective-permute-start.8 = (bf16[16,16,576]{2,1,0:T(8,128)(2,1)S(1)}, bf16[16,16,576]{2,1,0:T(8,128)(2,1)S(1)}, u32[]{:S(2)}, u32[]{:S(2)}) collective-permute-start(bf16[16,16,576]{2,1,0:T(8,128)(2,1)S(1)} %collective-permute-done.7.refs_6_), channel_id=1, source_target_pairs={{0,112},{1,15},{2,114},{3,1},{4,116},{5,3},{6,118},{7,5},{8,120},{... | collective-permute-start | bytes 884744 | tf_op jit(solution)/shard_map/ppermute | solution.py:42
  57.2 7.1 %stage.1.sorted_keys = bf16[4,1024,576]{2,1,0:T(8,128)(2,1)} custom-call(s32[1]{0:T(128)} %bitcast.core_ref, s32[64]{0:T(128)S(1)} %select_reduce_fusion.label_ref, bf16[32,64,576]{2,1,0:T(8,128)(2,1)} %own_pool.1, bf16[32,64,576]{2,1,0:T(8,128)(2,1)S(1)} %collective-permute-done.1.other_pool), custom_call_target="tpu_custom_call" | custom-call | flops 4000000000 | tf_op jit(solution)/shard_map/stage/pallas_call | solution.py:247
  64.4 15.4 %attend.1 = (f32[17,16,512]{2,1,0:T(8,128)S(1)}, bf16[17,16,512]{2,1,0:T(8,128)(2,1)S(1)}, bf16[17,16,512]{2,1,0:T(8,128)(2,1)S(1)}, bf16[17,16,512]{2,1,0:T(8,1...) custom-call(s32[1]{0:T(128)} %bitcast.core_ref, ...), custom_call_target="tpu_custom_call" | custom-call | flops 9059696640 | tf_op jit(solution)/shard_map/attend/pallas_call | solution.py:272
  79.8 4.3 %collective-permute-start.11 = (bf16[17,16,512]{2,1,0:T(8,128)(2,1)S(1)}, bf16[17,16,512]{2,1,0:T(8,128)(2,1)S(1)}, u32[]{:S(2)}, u32[]{:S(2)}) collective-permute-start(bf16[17,16,512]{2,1,0:T(8,128)(2,1)S(1)} %get-tuple-element.18), channel_id=1, source_target_pairs={{0,64},{1,9},{2,66},{3,11},{4,68},{5,13},{6,70},{7,15},{8,72},{9,1... | collective-permute-start | bytes 835592 | tf_op jit(solution)/shard_map/ppermute | solution.py:42
  84.1 0.9 collective-permute-start.12
  85.0 4.1 %collective-permute-start.13 = (bf16[17,16,512]{2,1,0:T(8,128)(2,1)S(1)}, bf16[17,16,512]{2,1,0:T(8,128)(2,1)S(1)}, u32[]{:S(2)}, u32[]{:S(2)}) collective-permute-start(bf16[17,16,512]{2,1,0:T(8,128)(2,1)S(1)} %get-tuple-element.20), channel_id=1, source_target_pairs={{0,48},{1,7},{2,50},{3,9},{4,52},{5,11},{6,54},{7,13},{8,56},{9,15... | collective-permute-start | bytes 835592 | tf_op jit(solution)/shard_map/ppermute | solution.py:42
  89.2 4.1 %collective-permute-start.15 = (bf16[17,16,512]{2,1,0:T(8,128)(2,1)S(1)}, bf16[17,16,512]{2,1,0:T(8,128)(2,1)S(1)}, u32[]{:S(2)}, u32[]{:S(2)}) collective-permute-start(bf16[17,16,512]{2,1,0:T(8,128)(2,1)S(1)} %get-tuple-element.22), channel_id=1, source_target_pairs={{0,32},{1,5},{2,34},{3,7},{4,36},{5,9},{6,38},{7,11},{8,40},{9,13}... | collective-permute-start | bytes 835592 | tf_op jit(solution)/shard_map/ppermute | solution.py:42
  93.3 0.8 collective-permute-start.16
  94.1 8.0 %collective-permute-done.12.refs_2_ = bf16[17,16,512]{2,1,0:T(8,128)(2,1)S(1)} collective-permute-done((bf16[17,16,512]{2,1,0:T(8,128)(2,1)S(1)}, bf16[17,16,512]{2,1,0:T(8,128)(2,1)S(1)}, u32[]{:S(2)}, u32[]{:S(2)}) %collective-permute-start.12) | collective-permute-done | bytes 278560 | tf_op jit(solution)/shard_map/ppermute | solution.py:42
  102.1 6.0 %collective-permute-done.14.refs_4_ = bf16[17,16,512]{2,1,0:T(8,128)(2,1)S(1)} collective-permute-done((bf16[17,16,512]{2,1,0:T(8,128)(2,1)S(1)}, bf16[17,16,512]{2,1,0:T(8,128)(2,1)S(1)}, u32[]{:S(2)}, u32[]{:S(2)}) %collective-permute-start.14) | collective-permute-done | bytes 278560 | tf_op jit(solution)/shard_map/ppermute | solution.py:42
  108.1 3.0 %collective-permute-done.16.refs_6_ = bf16[17,16,512]{2,1,0:T(8,128)(2,1)S(1)} collective-permute-done((bf16[17,16,512]{2,1,0:T(8,128)(2,1)S(1)}, bf16[17,16,512]{2,1,0:T(8,128)(2,1)S(1)}, u32[]{:S(2)}, u32[]{:S(2)}) %collective-permute-start.16) | collective-permute-done | bytes 278560 | tf_op jit(solution)/shard_map/ppermute | solution.py:42
  111.1 0.7 merge.1
  111.8 21.0 %all_to_all.11.parts = f32[8,2,16,640]{3,2,1,0:T(8,128)S(1)} all-to-all(f32[8,2,16,640]{3,2,1,0:T(8,128)S(1)} %bitcast.14), channel_id=1, replica_groups={{0,2,4,6,8,10,12,14},{16,18,20,22,24,26,28,30},{32,34,36,38,40,42,44,46..., dimensions={0} | all-to-all | bytes 1310720 | tf_op jit(solution)/shard_map/all_to_all | solution.py:347
  132.8 0.2 finish.1
  133.0 0.1 collective-permute-start.18
  133.2 1.2 collective-permute-done.18
  134.3 0.6 maximum_select_fusion
  (29 shorter events, 0.4 us)
Async XLA Ops:
  0.0 64.4 %collective-permute-start.2 = (bf16[32,576,128]{2,1,0:T(8,128)(2,1)}, bf16[32,576,128]{2,1,0:T(8,128)(2,1)}, u32[]{:S(2)}, u32[]{:S(2)}) collective-permute-start(bf16[32,576,128]{2,1,0:T(8,128)(2,1)} %bitcast.23), channel_id=1, source_target_pairs={{0,1},{1,0},{2,3},{3,2},{4,5},{5,4},{6,7},{7,6},{8,9},{9,8},{10,11... | collective-permute-start | bytes 14155784 | tf_op jit(solution)/shard_map/ppermute | solution.py:45
  0.8 7.5 %collective-permute-start = (bf16[16,576]{1,0:T(8,128)(2,1)S(1)}, bf16[16,576]{1,0:T(8,128)(2,1)S(1)}, u32[]{:S(2)}, u32[]{:S(2)}) collective-permute-start(bf16[16,576]{1,0:T(8,128)(2,1)S(1)} %get-tuple-element.26), channel_id=1, source_target_pairs={{0,1},{1,0},{2,3},{3,2},{4,5},{5,4},{6,7},{7,6},{8,9},{9,8},{10,11... | collective-permute-start | bytes 55304 | tf_op jit(solution)/shard_map/ppermute | solution.py:45
  8.3 46.9 %collective-permute-start.1 = (bf16[32,64,576]{2,1,0:T(8,128)(2,1)}, bf16[32,64,576]{2,1,0:T(8,128)(2,1)S(1)}, u32[]{:S(2)}, u32[]{:S(2)}) collective-permute-start(bf16[32,64,576]{2,1,0:T(8,128)(2,1)} %own_pool.1), channel_id=1, source_target_pairs={{0,1},{1,0},{2,3},{3,2},{4,5},{5,4},{6,7},{7,6},{8,9},{9,8},{10,11... | collective-permute-start | bytes 7077896 | tf_op jit(solution)/shard_map/ppermute | solution.py:45
  33.3 13.4 %collective-permute-start.7 = (bf16[16,16,576]{2,1,0:T(8,128)(2,1)S(1)}, bf16[16,16,576]{2,1,0:T(8,128)(2,1)S(1)}, u32[]{:S(2)}, u32[]{:S(2)}) collective-permute-start(bf16[16,16,576]{2,1,0:T(8,128)(2,1)S(1)} %bitcast.15), channel_id=1, source_target_pairs={{0,96},{1,13},{2,98},{3,15},{4,100},{5,1},{6,102},{7,3},{8,104},{9... | collective-permute-start | bytes 884744 | tf_op jit(solution)/shard_map/ppermute | solution.py:42
  42.8 8.1 %collective-permute-start.4 = (bf16[16,16,576]{2,1,0:T(8,128)(2,1)S(1)}, bf16[16,16,576]{2,1,0:T(8,128)(2,1)S(1)}, u32[]{:S(2)}, u32[]{:S(2)}) collective-permute-start(bf16[16,16,576]{2,1,0:T(8,128)(2,1)S(1)} %bitcast.16), channel_id=1, source_target_pairs={{0,32},{1,5},{2,34},{3,7},{4,36},{5,9},{6,38},{7,11},{8,40},{9,13}... | collective-permute-start | bytes 884744 | tf_op jit(solution)/shard_map/ppermute | solution.py:42
  42.8 10.6 %collective-permute-start.3 = (bf16[16,16,576]{2,1,0:T(8,128)(2,1)S(1)}, bf16[16,16,576]{2,1,0:T(8,128)(2,1)S(1)}, u32[]{:S(2)}, u32[]{:S(2)}) collective-permute-start(bf16[16,16,576]{2,1,0:T(8,128)(2,1)S(1)} %bitcast.17), channel_id=1, source_target_pairs={{0,16},{1,3},{2,18},{3,5},{4,20},{5,7},{6,22},{7,9},{8,24},{9,11},... | collective-permute-start | bytes 884744 | tf_op jit(solution)/shard_map/ppermute | solution.py:42
  46.6 8.5 %collective-permute-start.9 = (bf16[16,16,576]{2,1,0:T(8,128)(2,1)S(1)}, bf16[16,16,576]{2,1,0:T(8,128)(2,1)S(1)}, u32[]{:S(2)}, u32[]{:S(2)}) collective-permute-start(bf16[16,16,576]{2,1,0:T(8,128)(2,1)S(1)} %bitcast.18), channel_id=1, source_target_pairs={{0,112},{1,15},{2,114},{3,1},{4,116},{5,3},{6,118},{7,5},{8,120},{... | collective-permute-start | bytes 884744 | tf_op jit(solution)/shard_map/ppermute | solution.py:42
  50.8 13.5 %collective-permute-start.10 = (bf16[8,16,576]{2,1,0:T(8,128)(2,1)S(1)}, bf16[8,16,576]{2,1,0:T(8,128)(2,1)S(1)}, u32[]{:S(2)}, u32[]{:S(2)}) collective-permute-start(bf16[8,16,576]{2,1,0:T(8,128)(2,1)S(1)} %slice.18), channel_id=1, source_target_pairs={{0,96},{1,13},{2,98},{3,15},{4,100},{5,1},{6,102},{7,3},{8,104},{9... | collective-permute-start | bytes 442376 | tf_op jit(solution)/shard_map/ppermute | solution.py:42
  53.4 10.9 %collective-permute-start.6 = (bf16[8,16,576]{2,1,0:T(8,128)(2,1)S(1)}, bf16[8,16,576]{2,1,0:T(8,128)(2,1)S(1)}, u32[]{:S(2)}, u32[]{:S(2)}) collective-permute-start(bf16[8,16,576]{2,1,0:T(8,128)(2,1)S(1)} %slice.17), channel_id=1, source_target_pairs={{0,32},{1,5},{2,34},{3,7},{4,36},{5,9},{6,38},{7,11},{8,40},{9,13}... | collective-permute-start | bytes 442376 | tf_op jit(solution)/shard_map/ppermute | solution.py:42
  55.1 9.2 %collective-permute-start.5 = (bf16[16,16,576]{2,1,0:T(8,128)(2,1)S(1)}, bf16[16,16,576]{2,1,0:T(8,128)(2,1)S(1)}, u32[]{:S(2)}, u32[]{:S(2)}) collective-permute-start(bf16[16,16,576]{2,1,0:T(8,128)(2,1)S(1)} %collective-permute-done.4.refs_2_), channel_id=1, source_target_pairs={{0,16},{1,3},{2,18},{3,5},{4,20},{5,7},{6,22},{7,9},{8,24},{9,11},... | collective-permute-start | bytes 884744 | tf_op jit(solution)/shard_map/ppermute | solution.py:42
  55.1 9.2 %collective-permute-start.8 = (bf16[16,16,576]{2,1,0:T(8,128)(2,1)S(1)}, bf16[16,16,576]{2,1,0:T(8,128)(2,1)S(1)}, u32[]{:S(2)}, u32[]{:S(2)}) collective-permute-start(bf16[16,16,576]{2,1,0:T(8,128)(2,1)S(1)} %collective-permute-done.7.refs_6_), channel_id=1, source_target_pairs={{0,112},{1,15},{2,114},{3,1},{4,116},{5,3},{6,118},{7,5},{8,120},{... | collective-permute-start | bytes 884744 | tf_op jit(solution)/shard_map/ppermute | solution.py:42
  57.2 7.2 %copy-start = (s32[32]{0:T(128)S(1)}, s32[32]{0:T(128)}, u32[]{:S(2)}) copy-start(s32[32]{0:T(128)} %prefix_ref.1) | copy-start | bytes 388
  79.8 13.5 %collective-permute-start.11 = (bf16[17,16,512]{2,1,0:T(8,128)(2,1)S(1)}, bf16[17,16,512]{2,1,0:T(8,128)(2,1)S(1)}, u32[]{:S(2)}, u32[]{:S(2)}) collective-permute-start(bf16[17,16,512]{2,1,0:T(8,128)(2,1)S(1)} %get-tuple-element.18), channel_id=1, source_target_pairs={{0,64},{1,9},{2,66},{3,11},{4,68},{5,13},{6,70},{7,15},{8,72},{9,1... | collective-permute-start | bytes 835592 | tf_op jit(solution)/shard_map/ppermute | solution.py:42
  84.1 18.0 %collective-permute-start.12 = (bf16[17,16,512]{2,1,0:T(8,128)(2,1)S(1)}, bf16[17,16,512]{2,1,0:T(8,128)(2,1)S(1)}, u32[]{:S(2)}, u32[]{:S(2)}) collective-permute-start(bf16[17,16,512]{2,1,0:T(8,128)(2,1)S(1)} %get-tuple-element.19), channel_id=1, source_target_pairs={{0,80},{1,11},{2,82},{3,13},{4,84},{5,15},{6,86},{7,1},{8,88},{9,3... | collective-permute-start | bytes 835592 | tf_op jit(solution)/shard_map/ppermute | solution.py:42
  85.0 17.1 %collective-permute-start.13 = (bf16[17,16,512]{2,1,0:T(8,128)(2,1)S(1)}, bf16[17,16,512]{2,1,0:T(8,128)(2,1)S(1)}, u32[]{:S(2)}, u32[]{:S(2)}) collective-permute-start(bf16[17,16,512]{2,1,0:T(8,128)(2,1)S(1)} %get-tuple-element.20), channel_id=1, source_target_pairs={{0,48},{1,7},{2,50},{3,9},{4,52},{5,11},{6,54},{7,13},{8,56},{9,15... | collective-permute-start | bytes 835592 | tf_op jit(solution)/shard_map/ppermute | solution.py:42
  89.2 18.9 %collective-permute-start.14 = (bf16[17,16,512]{2,1,0:T(8,128)(2,1)S(1)}, bf16[17,16,512]{2,1,0:T(8,128)(2,1)S(1)}, u32[]{:S(2)}, u32[]{:S(2)}) collective-permute-start(bf16[17,16,512]{2,1,0:T(8,128)(2,1)S(1)} %get-tuple-element.21), channel_id=1, source_target_pairs={{0,96},{1,13},{2,98},{3,15},{4,100},{5,1},{6,102},{7,3},{8,104},{9... | collective-permute-start | bytes 835592 | tf_op jit(solution)/shard_map/ppermute | solution.py:42
  89.2 18.9 %collective-permute-start.15 = (bf16[17,16,512]{2,1,0:T(8,128)(2,1)S(1)}, bf16[17,16,512]{2,1,0:T(8,128)(2,1)S(1)}, u32[]{:S(2)}, u32[]{:S(2)}) collective-permute-start(bf16[17,16,512]{2,1,0:T(8,128)(2,1)S(1)} %get-tuple-element.22), channel_id=1, source_target_pairs={{0,32},{1,5},{2,34},{3,7},{4,36},{5,9},{6,38},{7,11},{8,40},{9,13}... | collective-permute-start | bytes 835592 | tf_op jit(solution)/shard_map/ppermute | solution.py:42
  93.3 17.8 %collective-permute-start.16 = (bf16[17,16,512]{2,1,0:T(8,128)(2,1)S(1)}, bf16[17,16,512]{2,1,0:T(8,128)(2,1)S(1)}, u32[]{:S(2)}, u32[]{:S(2)}) collective-permute-start(bf16[17,16,512]{2,1,0:T(8,128)(2,1)S(1)} %get-tuple-element.23), channel_id=1, source_target_pairs={{0,112},{1,15},{2,114},{3,1},{4,116},{5,3},{6,118},{7,5},{8,120},{... | collective-permute-start | bytes 835592 | tf_op jit(solution)/shard_map/ppermute | solution.py:42
  102.1 9.0 %collective-permute-start.17 = (bf16[17,16,512]{2,1,0:T(8,128)(2,1)S(1)}, bf16[17,16,512]{2,1,0:T(8,128)(2,1)S(1)}, u32[]{:S(2)}, u32[]{:S(2)}) collective-permute-start(bf16[17,16,512]{2,1,0:T(8,128)(2,1)S(1)} %get-tuple-element.24), channel_id=1, source_target_pairs={{0,16},{1,3},{2,18},{3,5},{4,20},{5,7},{6,22},{7,9},{8,24},{9,11},... | collective-permute-start | bytes 835592 | tf_op jit(solution)/shard_map/ppermute | solution.py:42
  133.0 1.3 collective-permute-start.18

commit v2 on v1

--- a/solution.py
+++ b/solution.py
@@ -10,6 +10,7 @@
 
 
 LAT = 512
+LANES = 128
 PARTS = 2
 WIDE = 2
 CORES = 2
@@ -75,7 +76,7 @@
 
 
 def attend_kernel(core_ref, prefix_ref, live_ref, sorted_keys, own_suffix, other_suffix, *refs):
-    *refs, keys, tails, stat_m, stat_l, heads, members, counts, key_sems, tail_sems = refs
+    *refs, keys, tails, stats, heads, members, counts, key_sems, tail_sems = refs
     n = len(refs) // 2
     halved = n // 2
     half = prefix_ref.shape[0] // CORES // 2
@@ -83,7 +84,8 @@
     prefixes = keys.shape[0]
     requests, _, spots = tails.shape
     slots = spots // CORES
-    per = outs[0].shape[1]
+    per = blocks[0].shape[1]
+    wide_tiles = LAT // LANES
     total = n * per
     core = core_ref[0]
 
@@ -116,8 +118,7 @@
         return carry
 
     lax.fori_loop(0, prefixes, load, 0)
-    stat_m[...] = jnp.zeros_like(stat_m)
-    stat_l[...] = jnp.ones_like(stat_l)
+    stats[...] = jnp.zeros_like(stats)
     nt = (((1,), (1,)), ((), ()))
 
     def fetch(r, base):
@@ -185,10 +186,15 @@
             t = lax.dot_general(split(w), tails[r, :LAT], nt, preferred_element_type=jnp.float32)
             res = o[here] + t[:total] + t[total:]
             for k in range(n):
-                outs[k][r] = res[k * per : (k + 1) * per].astype(outs[k].dtype)
-            lane = lax.broadcasted_iota(jnp.int32, stat_m.shape, 1)
-            stat_m[...] = jnp.where(lane == r, top[here], stat_m[...])
-            stat_l[...] = jnp.where(lane == r, l, stat_l[...])
+                for t in range(wide_tiles):
+                    tile = res[k * per : (k + 1) * per, t * LANES : (t + 1) * LANES]
+                    span = pl.ds((r * wide_tiles + t) * per, per)
+                    outs[k][span] = tile.astype(outs[k].dtype)
+            lane = lax.broadcasted_iota(jnp.int32, stats.shape, 1)
+            high = l.astype(jnp.bfloat16).astype(jnp.float32)
+            new = jnp.where(lane == r, top[here], stats[...])
+            new = jnp.where(lane == requests + r, high, new)
+            stats[...] = jnp.where(lane == 2 * requests + r, l - high, new)
 
     def prefix(p, carry):
         key_copy(p).wait()
@@ -198,31 +204,29 @@
     lax.fori_loop(0, prefixes, prefix, 0)
 
     for k in range(n):
-        here = slice(k * per, (k + 1) * per)
-        l = stat_l[here]
-        high = l.astype(jnp.bfloat16).astype(jnp.float32)
-        parts = [stat_m[here], high, l - high, jnp.zeros_like(l)]
-        outs[k][requests] = jnp.concatenate(parts, axis=1).astype(outs[k].dtype)
+        outs[k][pl.ds(requests * wide_tiles * per, per)] = stats[k * per : (k + 1) * per].astype(outs[k].dtype)
 
 
 def merge_kernel(*refs):
     parts, out = refs[:-1], refs[-1]
-    requests = parts[0].shape[0] - 1
-    per = parts[0].shape[1]
-    stats = [p[requests].astype(jnp.float32) for p in parts]
-    lanes = 128
-    tops = [s[:, :lanes] for s in stats]
-    sums = [s[:, lanes : 2 * lanes] + s[:, 2 * lanes : 3 * lanes] for s in stats]
+    per, requests, _ = out.shape
+    tiles = LAT // LANES
+    stats = [p[requests * tiles * per : (requests * tiles + 1) * per].astype(jnp.float32) for p in parts]
+    tops = [s[:, :requests] for s in stats]
+    sums = [s[:, requests : 2 * requests] + s[:, 2 * requests : 3 * requests] for s in stats]
     top = functools.reduce(jnp.maximum, tops)
     scales = [jnp.exp2((t - top) * LOG2_SCALE) for t in tops]
     l = functools.reduce(jnp.add, [s * f for s, f in zip(sums, scales)])
-    lane = lax.broadcasted_iota(jnp.int32, (per, lanes), 1)
+    lane = lax.broadcasted_iota(jnp.int32, (per, LANES), 1)
     for r in range(requests):
-        acc = None
-        for part, f in zip(parts, scales):
-            term = part[r].astype(jnp.float32) * f[:, r : r + 1]
-            acc = term if acc is None else acc + term
-        out[:, r, :LAT] = acc
+        columns = [f[:, r : r + 1] for f in scales]
+        for t in range(tiles):
+            acc = None
+            for part, f in zip(parts, columns):
+                first = (r * tiles + t) * per
+                term = part[first : first + per].astype(jnp.float32) * f
+                acc = term if acc is None else acc + term
+            out[:, r, t * LANES : (t + 1) * LANES] = acc
         out[:, r, LAT:] = jnp.where(lane == 0, top[:, r : r + 1], l[:, r : r + 1])
 
 
@@ -271,14 +275,13 @@
     )
     return pl.pallas_call(
         attend_kernel,
-        out_shape=[jax.ShapeDtypeStruct((half + 1, per, LAT), t) for t in dtypes],
+        out_shape=[jax.ShapeDtypeStruct(((half * (LAT // LANES) + 1) * per, LANES), t) for t in dtypes],
         in_specs=[SMEM] * 3 + [ANY] * 3 + [VMEM] * len(blocks),
         out_specs=[VMEM] * n,
         scratch_shapes=[
             pltpu.VMEM(keys.shape, jnp.bfloat16),
             pltpu.VMEM(tails, jnp.bfloat16),
-            pltpu.VMEM((n * per, 128), jnp.float32),
-            pltpu.VMEM((n * per, 128), jnp.float32),
+            pltpu.VMEM((n * per, LANES), jnp.float32),
             pltpu.VMEM((WIDE * n * per, channels), jnp.bfloat16),
             pltpu.SMEM((prefixes * half,), jnp.int32),
             pltpu.SMEM((prefixes,), jnp.int32),

time: 137 us -> 137 us (level)
  no operation moved by 1% of the time
where the time goes in v2:
time: 137 us; the launch traced here: 134 us
  blocking collectives  45.2 us (33%)
  waiting for transfers between devices  32.2 us (24%)
  starting transfers between devices  28.9 us (21%)
  Pallas kernels  23.7 us (17%)
  other arithmetic  2.47 us (2%)
  local copies, waits for them, and re-layouts  1.47 us (1%)
    ppermute x15, starting transfers between devices, shift(): return lax.ppermute(value, 'seq', pairs)  28.2 us
    all_to_all x1, blocking collectives, body(): lax.all_to_all(spread, 'seq', 0, 0, axis_index_groups=torus.groups(True))  24.1 us
    ppermute x15, waiting for transfers between devices, shift(): return lax.ppermute(value, 'seq', pairs)  24 us
    all_to_all x1, blocking collectives, body(): lax.all_to_all(merged.reshape(side, CORES, half, LAT + 128), 'seq', 0, 0,...  21.1 us
    pallas_call x1, Pallas kernels, attend(): pl.pallas_call(attend_kernel, out_shape=[jax.ShapeDtypeStruct(((half * (L...  15.5 us
    ppermute x4, waiting for transfers between devices, partner(): return lax.ppermute(value, 'seq', [(i, i ^ 1) for i in range(self.devices)])  8.15 us
    pallas_call x1, Pallas kernels, stage(): pl.pallas_call(stage_kernel, out_shape=pltpu.HBM(keys, jnp.bfloat16), in_...  7.15 us
  transfers between devices with their start and end apart: 19, of which 8 were waited for; matrix products, arithmetic and copies ran while one was open for 2% of the time, Pallas kernels for 5%

profile of v2, /device:TPU:516, one launch (start us, length us, event | category | flops | bytes accessed | tf_op | source)
XLA Modules:
  0.0 134.1 jit_solution(15250857027524555587)
XLA Ops:
  0.0 0.7 constant_dynamic-slice_fusion
  0.8 0.5 collective-permute-start
  1.3 7.0 %collective-permute-done = bf16[16,576]{1,0:T(8,128)(2,1)S(1)} collective-permute-done((bf16[16,576]{1,0:T(8,128)(2,1)S(1)}, bf16[16,576]{1,0:T(8,128)(2,1)S(1)}, u32[]{:S(2)}, u32[]{:S(2)}) %collective-permute-start) | collective-permute-done | bytes 18464 | tf_op jit(solution)/shard_map/ppermute | solution.py:46
  8.4 0.2 broadcast_in_dim.2
  8.6 24.1 %all_to_all.10 = bf16[8,2,16,576]{3,1,2,0:T(2,128)(2,1)S(1)} all-to-all(bf16[8,2,16,576]{3,1,2,0:T(2,128)(2,1)S(1)} %broadcast_in_dim.2), channel_id=1, replica_groups={{0,2,4,6,8,10,12,14},{16,18,20,22,24,26,28,30},{32,34,36,38,40,42,44,46..., dimensions={0} | all-to-all | bytes 589824 | tf_op jit(solution)/shard_map/all_to_all | solution.py:323
  32.8 0.2 copy.13
  33.0 0.2 reshape.40
  33.3 8.8 %collective-permute-start.7 = (bf16[16,16,576]{2,1,0:T(8,128)(2,1)S(1)}, bf16[16,16,576]{2,1,0:T(8,128)(2,1)S(1)}, u32[]{:S(2)}, u32[]{:S(2)}) collective-permute-start(bf16[16,16,576]{2,1,0:T(8,128)(2,1)S(1)} %bitcast.15), channel_id=1, source_target_pairs={{0,96},{1,13},{2,98},{3,15},{4,100},{5,1},{6,102},{7,3},{8,104},{9... | collective-permute-start | bytes 884744 | tf_op jit(solution)/shard_map/ppermute | solution.py:43
  42.0 0.7 broadcast_subtract_fusion.1
  42.8 3.8 %collective-permute-done.7.refs_6_ = bf16[16,16,576]{2,1,0:T(8,128)(2,1)S(1)} collective-permute-done((bf16[16,16,576]{2,1,0:T(8,128)(2,1)S(1)}, bf16[16,16,576]{2,1,0:T(8,128)(2,1)S(1)}, u32[]{:S(2)}, u32[]{:S(2)}) %collective-permute-start.7) | collective-permute-done | bytes 294944 | tf_op jit(solution)/shard_map/ppermute | solution.py:43
  46.7 1.0 compare_reduce_fusion
  47.8 3.1 %collective-permute-done.4.refs_2_ = bf16[16,16,576]{2,1,0:T(8,128)(2,1)S(1)} collective-permute-done((bf16[16,16,576]{2,1,0:T(8,128)(2,1)S(1)}, bf16[16,16,576]{2,1,0:T(8,128)(2,1)S(1)}, u32[]{:S(2)}, u32[]{:S(2)}) %collective-permute-start.4) | collective-permute-done | bytes 294944 | tf_op jit(solution)/shard_map/ppermute | solution.py:43
  50.8 1.5 %collective-permute-start.10 = (bf16[8,16,576]{2,1,0:T(8,128)(2,1)S(1)}, bf16[8,16,576]{2,1,0:T(8,128)(2,1)S(1)}, u32[]{:S(2)}, u32[]{:S(2)}) collective-permute-start(bf16[8,16,576]{2,1,0:T(8,128)(2,1)S(1)} %slice.18), channel_id=1, source_target_pairs={{0,96},{1,13},{2,98},{3,15},{4,100},{5,1},{6,102},{7,3},{8,104},{9... | collective-permute-start | bytes 442376 | tf_op jit(solution)/shard_map/ppermute | solution.py:43
  52.3 1.1 collective-permute-done.3.refs_1_
  53.4 1.7 %collective-permute-start.6 = (bf16[8,16,576]{2,1,0:T(8,128)(2,1)S(1)}, bf16[8,16,576]{2,1,0:T(8,128)(2,1)S(1)}, u32[]{:S(2)}, u32[]{:S(2)}) collective-permute-start(bf16[8,16,576]{2,1,0:T(8,128)(2,1)S(1)} %slice.17), channel_id=1, source_target_pairs={{0,32},{1,5},{2,34},{3,7},{4,36},{5,9},{6,38},{7,11},{8,40},{9,13}... | collective-permute-start | bytes 442376 | tf_op jit(solution)/shard_map/ppermute | solution.py:43
  55.1 2.0 %collective-permute-start.8 = (bf16[16,16,576]{2,1,0:T(8,128)(2,1)S(1)}, bf16[16,16,576]{2,1,0:T(8,128)(2,1)S(1)}, u32[]{:S(2)}, u32[]{:S(2)}) collective-permute-start(bf16[16,16,576]{2,1,0:T(8,128)(2,1)S(1)} %collective-permute-done.7.refs_6_), channel_id=1, source_target_pairs={{0,112},{1,15},{2,114},{3,1},{4,116},{5,3},{6,118},{7,5},{8,120},{... | collective-permute-start | bytes 884744 | tf_op jit(solution)/shard_map/ppermute | solution.py:43
  57.2 7.1 %stage.1.sorted_keys = bf16[4,1024,576]{2,1,0:T(8,128)(2,1)} custom-call(s32[1]{0:T(128)} %bitcast.core_ref, s32[64]{0:T(128)S(1)} %select_reduce_fusion.label_ref, bf16[32,64,576]{2,1,0:T(8,128)(2,1)} %own_pool.1, bf16[32,64,576]{2,1,0:T(8,128)(2,1)S(1)} %collective-permute-done.1.other_pool), custom_call_target="tpu_custom_call" | custom-call | flops 4000000000 | tf_op jit(solution)/shard_map/stage/pallas_call | solution.py:251
  64.4 15.5 %attend.1 = (f32[1040,128]{1,0:T(8,128)S(1)}, bf16[1040,128]{1,0:T(8,128)(2,1)S(1)}, bf16[1040,128]{1,0:T(8,128)(2,1)S(1)}, bf16[1040,128]{1,0:T(8,128)(2,1)S(1)...) custom-call(s32[1]{0:T(128)} %bitcast.core_ref, ...), custom_call_target="tpu_custom_call" | custom-call | flops 9059696640 | tf_op jit(solution)/shard_map/attend/pallas_call | solution.py:276
  79.9 4.3 %collective-permute-start.11 = (bf16[1040,128]{1,0:T(8,128)(2,1)S(1)}, bf16[1040,128]{1,0:T(8,128)(2,1)S(1)}, u32[]{:S(2)}, u32[]{:S(2)}) collective-permute-start(bf16[1040,128]{1,0:T(8,128)(2,1)S(1)} %get-tuple-element.18), channel_id=1, source_target_pairs={{0,64},{1,9},{2,66},{3,11},{4,68},{5,13},{6,70},{7,15},{8,72},{9,1... | collective-permute-start | bytes 798728 | tf_op jit(solution)/shard_map/ppermute | solution.py:43
  84.2 0.9 collective-permute-start.12
  85.0 4.2 %collective-permute-start.13 = (bf16[1040,128]{1,0:T(8,128)(2,1)S(1)}, bf16[1040,128]{1,0:T(8,128)(2,1)S(1)}, u32[]{:S(2)}, u32[]{:S(2)}) collective-permute-start(bf16[1040,128]{1,0:T(8,128)(2,1)S(1)} %get-tuple-element.20), channel_id=1, source_target_pairs={{0,48},{1,7},{2,50},{3,9},{4,52},{5,11},{6,54},{7,13},{8,56},{9,15... | collective-permute-start | bytes 798728 | tf_op jit(solution)/shard_map/ppermute | solution.py:43
  89.2 4.1 %collective-permute-start.15 = (bf16[1040,128]{1,0:T(8,128)(2,1)S(1)}, bf16[1040,128]{1,0:T(8,128)(2,1)S(1)}, u32[]{:S(2)}, u32[]{:S(2)}) collective-permute-start(bf16[1040,128]{1,0:T(8,128)(2,1)S(1)} %get-tuple-element.22), channel_id=1, source_target_pairs={{0,32},{1,5},{2,34},{3,7},{4,36},{5,9},{6,38},{7,11},{8,40},{9,13}... | collective-permute-start | bytes 798728 | tf_op jit(solution)/shard_map/ppermute | solution.py:43
  93.3 0.6 collective-permute-start.16
  94.0 7.6 %collective-permute-done.12.refs_2_ = bf16[1040,128]{1,0:T(8,128)(2,1)S(1)} collective-permute-done((bf16[1040,128]{1,0:T(8,128)(2,1)S(1)}, bf16[1040,128]{1,0:T(8,128)(2,1)S(1)}, u32[]{:S(2)}, u32[]{:S(2)}) %collective-permute-start.12) | collective-permute-done | bytes 266272 | tf_op jit(solution)/shard_map/ppermute | solution.py:43
  101.5 5.7 %collective-permute-done.14.refs_4_ = bf16[1040,128]{1,0:T(8,128)(2,1)S(1)} collective-permute-done((bf16[1040,128]{1,0:T(8,128)(2,1)S(1)}, bf16[1040,128]{1,0:T(8,128)(2,1)S(1)}, u32[]{:S(2)}, u32[]{:S(2)}) %collective-permute-start.14) | collective-permute-done | bytes 266272 | tf_op jit(solution)/shard_map/ppermute | solution.py:43
  107.2 2.8 %collective-permute-done.16.refs_6_ = bf16[1040,128]{1,0:T(8,128)(2,1)S(1)} collective-permute-done((bf16[1040,128]{1,0:T(8,128)(2,1)S(1)}, bf16[1040,128]{1,0:T(8,128)(2,1)S(1)}, u32[]{:S(2)}, u32[]{:S(2)}) %collective-permute-start.16) | collective-permute-done | bytes 266272 | tf_op jit(solution)/shard_map/ppermute | solution.py:43
  110.1 0.9 merge.1
  110.9 21.1 %all_to_all.11.parts = f32[8,2,16,640]{3,2,1,0:T(8,128)S(1)} all-to-all(f32[8,2,16,640]{3,2,1,0:T(8,128)S(1)} %bitcast.14), channel_id=1, replica_groups={{0,2,4,6,8,10,12,14},{16,18,20,22,24,26,28,30},{32,34,36,38,40,42,44,46..., dimensions={0} | all-to-all | bytes 1310720 | tf_op jit(solution)/shard_map/all_to_all | solution.py:350
  132.0 0.2 finish.1
  132.2 0.1 collective-permute-start.18
  132.4 1.2 collective-permute-done.18
  133.5 0.6 maximum_select_fusion
  (29 shorter events, 0.4 us)
Async XLA Ops:
  0.0 64.4 %collective-permute-start.2 = (bf16[32,576,128]{2,1,0:T(8,128)(2,1)}, bf16[32,576,128]{2,1,0:T(8,128)(2,1)}, u32[]{:S(2)}, u32[]{:S(2)}) collective-permute-start(bf16[32,576,128]{2,1,0:T(8,128)(2,1)} %bitcast.23), channel_id=1, source_target_pairs={{0,1},{1,0},{2,3},{3,2},{4,5},{5,4},{6,7},{7,6},{8,9},{9,8},{10,11... | collective-permute-start | bytes 14155784 | tf_op jit(solution)/shard_map/ppermute | solution.py:46
  0.8 7.5 %collective-permute-start = (bf16[16,576]{1,0:T(8,128)(2,1)S(1)}, bf16[16,576]{1,0:T(8,128)(2,1)S(1)}, u32[]{:S(2)}, u32[]{:S(2)}) collective-permute-start(bf16[16,576]{1,0:T(8,128)(2,1)S(1)} %get-tuple-element.26), channel_id=1, source_target_pairs={{0,1},{1,0},{2,3},{3,2},{4,5},{5,4},{6,7},{7,6},{8,9},{9,8},{10,11... | collective-permute-start | bytes 55304 | tf_op jit(solution)/shard_map/ppermute | solution.py:46
  8.3 46.9 %collective-permute-start.1 = (bf16[32,64,576]{2,1,0:T(8,128)(2,1)}, bf16[32,64,576]{2,1,0:T(8,128)(2,1)S(1)}, u32[]{:S(2)}, u32[]{:S(2)}) collective-permute-start(bf16[32,64,576]{2,1,0:T(8,128)(2,1)} %own_pool.1), channel_id=1, source_target_pairs={{0,1},{1,0},{2,3},{3,2},{4,5},{5,4},{6,7},{7,6},{8,9},{9,8},{10,11... | collective-permute-start | bytes 7077896 | tf_op jit(solution)/shard_map/ppermute | solution.py:46
  33.3 13.4 %collective-permute-start.7 = (bf16[16,16,576]{2,1,0:T(8,128)(2,1)S(1)}, bf16[16,16,576]{2,1,0:T(8,128)(2,1)S(1)}, u32[]{:S(2)}, u32[]{:S(2)}) collective-permute-start(bf16[16,16,576]{2,1,0:T(8,128)(2,1)S(1)} %bitcast.15), channel_id=1, source_target_pairs={{0,96},{1,13},{2,98},{3,15},{4,100},{5,1},{6,102},{7,3},{8,104},{9... | collective-permute-start | bytes 884744 | tf_op jit(solution)/shard_map/ppermute | solution.py:43
  42.8 8.1 %collective-permute-start.4 = (bf16[16,16,576]{2,1,0:T(8,128)(2,1)S(1)}, bf16[16,16,576]{2,1,0:T(8,128)(2,1)S(1)}, u32[]{:S(2)}, u32[]{:S(2)}) collective-permute-start(bf16[16,16,576]{2,1,0:T(8,128)(2,1)S(1)} %bitcast.16), channel_id=1, source_target_pairs={{0,32},{1,5},{2,34},{3,7},{4,36},{5,9},{6,38},{7,11},{8,40},{9,13}... | collective-permute-start | bytes 884744 | tf_op jit(solution)/shard_map/ppermute | solution.py:43
  42.8 10.6 %collective-permute-start.3 = (bf16[16,16,576]{2,1,0:T(8,128)(2,1)S(1)}, bf16[16,16,576]{2,1,0:T(8,128)(2,1)S(1)}, u32[]{:S(2)}, u32[]{:S(2)}) collective-permute-start(bf16[16,16,576]{2,1,0:T(8,128)(2,1)S(1)} %bitcast.17), channel_id=1, source_target_pairs={{0,16},{1,3},{2,18},{3,5},{4,20},{5,7},{6,22},{7,9},{8,24},{9,11},... | collective-permute-start | bytes 884744 | tf_op jit(solution)/shard_map/ppermute | solution.py:43
  46.6 8.5 %collective-permute-start.9 = (bf16[16,16,576]{2,1,0:T(8,128)(2,1)S(1)}, bf16[16,16,576]{2,1,0:T(8,128)(2,1)S(1)}, u32[]{:S(2)}, u32[]{:S(2)}) collective-permute-start(bf16[16,16,576]{2,1,0:T(8,128)(2,1)S(1)} %bitcast.18), channel_id=1, source_target_pairs={{0,112},{1,15},{2,114},{3,1},{4,116},{5,3},{6,118},{7,5},{8,120},{... | collective-permute-start | bytes 884744 | tf_op jit(solution)/shard_map/ppermute | solution.py:43
  50.8 13.5 %collective-permute-start.10 = (bf16[8,16,576]{2,1,0:T(8,128)(2,1)S(1)}, bf16[8,16,576]{2,1,0:T(8,128)(2,1)S(1)}, u32[]{:S(2)}, u32[]{:S(2)}) collective-permute-start(bf16[8,16,576]{2,1,0:T(8,128)(2,1)S(1)} %slice.18), channel_id=1, source_target_pairs={{0,96},{1,13},{2,98},{3,15},{4,100},{5,1},{6,102},{7,3},{8,104},{9... | collective-permute-start | bytes 442376 | tf_op jit(solution)/shard_map/ppermute | solution.py:43
  53.4 10.9 %collective-permute-start.6 = (bf16[8,16,576]{2,1,0:T(8,128)(2,1)S(1)}, bf16[8,16,576]{2,1,0:T(8,128)(2,1)S(1)}, u32[]{:S(2)}, u32[]{:S(2)}) collective-permute-start(bf16[8,16,576]{2,1,0:T(8,128)(2,1)S(1)} %slice.17), channel_id=1, source_target_pairs={{0,32},{1,5},{2,34},{3,7},{4,36},{5,9},{6,38},{7,11},{8,40},{9,13}... | collective-permute-start | bytes 442376 | tf_op jit(solution)/shard_map/ppermute | solution.py:43
  55.1 9.2 %collective-permute-start.5 = (bf16[16,16,576]{2,1,0:T(8,128)(2,1)S(1)}, bf16[16,16,576]{2,1,0:T(8,128)(2,1)S(1)}, u32[]{:S(2)}, u32[]{:S(2)}) collective-permute-start(bf16[16,16,576]{2,1,0:T(8,128)(2,1)S(1)} %collective-permute-done.4.refs_2_), channel_id=1, source_target_pairs={{0,16},{1,3},{2,18},{3,5},{4,20},{5,7},{6,22},{7,9},{8,24},{9,11},... | collective-permute-start | bytes 884744 | tf_op jit(solution)/shard_map/ppermute | solution.py:43
  55.1 9.2 %collective-permute-start.8 = (bf16[16,16,576]{2,1,0:T(8,128)(2,1)S(1)}, bf16[16,16,576]{2,1,0:T(8,128)(2,1)S(1)}, u32[]{:S(2)}, u32[]{:S(2)}) collective-permute-start(bf16[16,16,576]{2,1,0:T(8,128)(2,1)S(1)} %collective-permute-done.7.refs_6_), channel_id=1, source_target_pairs={{0,112},{1,15},{2,114},{3,1},{4,116},{5,3},{6,118},{7,5},{8,120},{... | collective-permute-start | bytes 884744 | tf_op jit(solution)/shard_map/ppermute | solution.py:43
  57.2 7.2 %copy-start = (s32[32]{0:T(128)S(1)}, s32[32]{0:T(128)}, u32[]{:S(2)}) copy-start(s32[32]{0:T(128)} %prefix_ref.1) | copy-start | bytes 388
  79.9 13.5 %collective-permute-start.11 = (bf16[1040,128]{1,0:T(8,128)(2,1)S(1)}, bf16[1040,128]{1,0:T(8,128)(2,1)S(1)}, u32[]{:S(2)}, u32[]{:S(2)}) collective-permute-start(bf16[1040,128]{1,0:T(8,128)(2,1)S(1)} %get-tuple-element.18), channel_id=1, source_target_pairs={{0,64},{1,9},{2,66},{3,11},{4,68},{5,13},{6,70},{7,15},{8,72},{9,1... | collective-permute-start | bytes 798728 | tf_op jit(solution)/shard_map/ppermute | solution.py:43
  84.2 17.4 %collective-permute-start.12 = (bf16[1040,128]{1,0:T(8,128)(2,1)S(1)}, bf16[1040,128]{1,0:T(8,128)(2,1)S(1)}, u32[]{:S(2)}, u32[]{:S(2)}) collective-permute-start(bf16[1040,128]{1,0:T(8,128)(2,1)S(1)} %get-tuple-element.19), channel_id=1, source_target_pairs={{0,80},{1,11},{2,82},{3,13},{4,84},{5,15},{6,86},{7,1},{8,88},{9,3... | collective-permute-start | bytes 798728 | tf_op jit(solution)/shard_map/ppermute | solution.py:43
  85.0 16.5 %collective-permute-start.13 = (bf16[1040,128]{1,0:T(8,128)(2,1)S(1)}, bf16[1040,128]{1,0:T(8,128)(2,1)S(1)}, u32[]{:S(2)}, u32[]{:S(2)}) collective-permute-start(bf16[1040,128]{1,0:T(8,128)(2,1)S(1)} %get-tuple-element.20), channel_id=1, source_target_pairs={{0,48},{1,7},{2,50},{3,9},{4,52},{5,11},{6,54},{7,13},{8,56},{9,15... | collective-permute-start | bytes 798728 | tf_op jit(solution)/shard_map/ppermute | solution.py:43
  89.2 18.0 %collective-permute-start.14 = (bf16[1040,128]{1,0:T(8,128)(2,1)S(1)}, bf16[1040,128]{1,0:T(8,128)(2,1)S(1)}, u32[]{:S(2)}, u32[]{:S(2)}) collective-permute-start(bf16[1040,128]{1,0:T(8,128)(2,1)S(1)} %get-tuple-element.21), channel_id=1, source_target_pairs={{0,96},{1,13},{2,98},{3,15},{4,100},{5,1},{6,102},{7,3},{8,104},{9... | collective-permute-start | bytes 798728 | tf_op jit(solution)/shard_map/ppermute | solution.py:43
  89.2 18.0 %collective-permute-start.15 = (bf16[1040,128]{1,0:T(8,128)(2,1)S(1)}, bf16[1040,128]{1,0:T(8,128)(2,1)S(1)}, u32[]{:S(2)}, u32[]{:S(2)}) collective-permute-start(bf16[1040,128]{1,0:T(8,128)(2,1)S(1)} %get-tuple-element.22), channel_id=1, source_target_pairs={{0,32},{1,5},{2,34},{3,7},{4,36},{5,9},{6,38},{7,11},{8,40},{9,13}... | collective-permute-start | bytes 798728 | tf_op jit(solution)/shard_map/ppermute | solution.py:43
  93.3 16.7 %collective-permute-start.16 = (bf16[1040,128]{1,0:T(8,128)(2,1)S(1)}, bf16[1040,128]{1,0:T(8,128)(2,1)S(1)}, u32[]{:S(2)}, u32[]{:S(2)}) collective-permute-start(bf16[1040,128]{1,0:T(8,128)(2,1)S(1)} %get-tuple-element.23), channel_id=1, source_target_pairs={{0,112},{1,15},{2,114},{3,1},{4,116},{5,3},{6,118},{7,5},{8,120},{... | collective-permute-start | bytes 798728 | tf_op jit(solution)/shard_map/ppermute | solution.py:43
  101.5 8.5 %collective-permute-start.17 = (bf16[1040,128]{1,0:T(8,128)(2,1)S(1)}, bf16[1040,128]{1,0:T(8,128)(2,1)S(1)}, u32[]{:S(2)}, u32[]{:S(2)}) collective-permute-start(bf16[1040,128]{1,0:T(8,128)(2,1)S(1)} %get-tuple-element.24), channel_id=1, source_target_pairs={{0,16},{1,3},{2,18},{3,5},{4,20},{5,7},{6,22},{7,9},{8,24},{9,11},... | collective-permute-start | bytes 798728 | tf_op jit(solution)/shard_map/ppermute | solution.py:43
  132.2 1.3 collective-permute-start.18
